TPU v7x, 1024 devices: a whole 4x4x32 slice. The times are simulated.
1024 devices in a mesh: group: 2 (over core), row: 8 (over z_lo), col: 64 (over x, y, z_hi).
Axes of the slice: x: 4, y: 4, z: 32 (z_hi: 4, z_lo: 8; z = z_hi * 8 + z_lo), core: 2. Of those that a mesh axis runs over, the one named last changes fastest.
Arguments:
- velocity_hat: float32 [3, 2, 16, 512, 512], P(None, None, ('group', 'row'), 'col'), may hold values from -6 to 6
- scalar: float32 [16, 1024, 1024], P('group', 'col', 'row'), may hold values from -6 to 6
- tile_offset: int32 [1], replicated, may hold values from 0 to 511
Outputs:
- velocity_new: float32 [3, 2, 16, 512, 512], P(None, None, ('group', 'row'), 'col')
- scalar_new: float32 [16, 1024, 1024], P('group', 'col', 'row')
Inputs may be any that keep to these rules, and one draw needn't show every extreme that they name: `tile_offset`: one offset for every tile and plane.
All inputs are finite; a program needn't handle non-finite values.
Results may differ from a plain program's by a relative error of at most 0.000076.
Values sent between devices are 32-bit elements; how exact they have to be, the bound alone decides.
A program may use at most 32 MiB of HBM per device.

v0:
```python
import math

import jax
import jax.numpy as jnp
import numpy as np
from jax import lax
from jax.experimental import pallas as pl
from jax.experimental.pallas import tpu as pltpu
from jax.sharding import PartitionSpec as P

time_step = 0.25
viscosity = 2.0
diffusivity = 0.15
substep = 0.2
MESH = pl.DeviceIdType.MESH

N, NC, NL = 512, 64, 8
KEPT = [0, 1, 2, 3, 4, 5, 10, 11, 12, 13, 14, 15]
ORDER = KEPT + [6, 7, 8, 9]


def tables():
    unit = 1.0 / math.sqrt(N)
    wave = np.arange(N)
    wave = np.where(wave < N // 2, wave, wave - N) / (N // 2)
    eye = np.eye(8)
    c_natural = np.arange(64)
    c_zw = np.array([4 * w + z for z in range(4) for w in range(16)])
    c_kept = np.array([4 * w + z for z in range(4) for w in ORDER])
    rows = np.arange(64)

    def angle(left, right, length):
        return 2 * np.pi * ((left[:, None] * right[None, :]) % length) / length

    eighth = np.arange(8)
    turn = np.exp(1j * angle(eighth, eighth, 8)) * unit

    first = []
    for e in range(2):
        part = np.zeros((2, 4, 8, 2, 2, 8, 8))
        for m in range(4):
            for l in range(8):
                v = turn[2 * m + e, l]
                for j in range(8):
                    part[0, m, j, 0, 0, l, j] = v.real
                    part[1, m, j, 0, 0, l, j] = -v.imag
                    part[0, m, j, 0, 1, l, j] = v.imag
                    part[1, m, j, 0, 1, l, j] = v.real
        part[:, :, :, 1, 0] = -part[:, :, :, 0, 1]
        part[:, :, :, 1, 1] = part[:, :, :, 0, 0]
        first.append(part.reshape(64, 256))

    lane = np.arange(128)
    twist_y = angle(rows, (lane // 8) % 8, N)
    twist_x = angle(rows, lane % 8, N)

    mixed = np.zeros((2, 2, 8, 8, 2, 8, 8))
    forward = np.zeros((2, 8, 8, 2, 2, 8, 8))
    last = [np.zeros((2, 2, 8, 8, 2, 4, 8)) for _ in range(2)]
    for l in range(8):
        for j in range(8):
            for p in range(8):
                v = turn[j, p]
                for half in range(2):
                    mixed[0, 0, l, j, half, p, l] = v.real
                    mixed[0, 1, l, j, half, p, l] = -v.imag
                    mixed[1, 0, l, j, half, p, l] = -v.imag
                    mixed[1, 1, l, j, half, p, l] = -v.real
                forward[0, p, l, 0, 0, l, j] = v.real
                forward[0, p, l, 0, 1, l, j] = -v.imag
                forward[0, p, l, 1, 0, l, j] = v.imag
                forward[0, p, l, 1, 1, l, j] = v.real
            for m in range(4):
                for e in range(2):
                    v = turn[2 * m + e, l]
                    t = last[e]
                    t[0, 0, l, j, 0, m, j] = v.real
                    t[1, 1, l, j, 0, m, j] = v.real
                    t[0, 1, l, j, 0, m, j] = v.imag
                    t[1, 0, l, j, 0, m, j] = -v.imag
                    t[0, 1, l, j, 1, m, j] = v.real
                    t[1, 0, l, j, 1, m, j] = -v.real
                    t[0, 0, l, j, 1, m, j] = -v.imag
                    t[1, 1, l, j, 1, m, j] = -v.imag
    forward_y = np.zeros_like(forward)
    forward_y[1] = forward[0]

    def pair(order):
        t = angle(order, rows, 64)
        return np.concatenate([np.cos(t), np.sin(t)], axis=1)

    stacked = angle(rows, c_zw, 64)
    kappa_y = np.zeros((2, 64, 2, 4, 8))
    for e in range(2):
        for m in range(4):
            kappa_y[e, :, :, m, :] = wave[64 * (2 * m + e) + rows][:, None, None]
    kappa_x = wave[8 * c_zw[:, None] + (lane % 8)[None, :]]

    spread = np.zeros((128, 256))
    for f in range(-2, 130):
        k = f // 2 + 1
        if f % 2 == 0:
            spread[k, f % 256] = 1.0
        else:
            spread[k, f % 256] = 0.5
            spread[k + 1, f % 256] = 0.5
    lift = np.zeros((2, 24, 24))
    for v in range(2):
        def slot(row):
            if row < 0:
                return 20 + v
            return 8 * v + row if row < 8 else 16 + 2 * v + row - 8
        for f in range(-2, 18):
            k = f // 2
            if f % 2 == 0:
                lift[v, f + 4, slot(k)] = 1.0
            else:
                lift[v, f + 4, slot(k)] = 0.5
                lift[v, f + 4, slot(k + 1)] = 0.5

    out = dict(
        first0=first[0], first1=first[1],
        tyc=np.cos(twist_y), tys=np.sin(twist_y), txc=np.cos(twist_x), txs=np.sin(twist_x),
        cs1=pair(c_natural), cs3=np.concatenate([np.cos(stacked).T, np.sin(stacked).T]).reshape(2, 64, 64).transpose(0, 1, 2).reshape(128, 64),
        mixed=mixed.reshape(256, 128), fx=forward.reshape(128, 256), fy=forward_y.reshape(128, 256),
        cs4=pair(c_kept), last0=last[0].reshape(256, 64), last1=last[1].reshape(256, 64),
        ky=kappa_y.reshape(128, 64), kx=kappa_x, spread=spread, lift=lift.reshape(48, 24),
    )
    flat = angle(rows, c_zw, 64)
    out["cs3"] = np.concatenate([np.cos(flat), np.sin(flat)], axis=0)
    return {k: np.asarray(v, np.float32) for k, v in out.items()}


NAMES = ["first0", "first1", "tyc", "tys", "txc", "txs", "cs1", "cs3", "mixed", "fx", "fy", "cs4",
         "last0", "last1", "ky", "kx", "spread", "lift"]


def dot(a, b):
    return jnp.dot(a, b, precision=lax.Precision.HIGHEST, preferred_element_type=jnp.float32)


def inverse_y(t, spectra, kappa_x):
    turned = []
    for comp in range(3):
        stacked = jnp.concatenate(
            [spectra(comp, ri)[:, 128 * m : 128 * m + 128] for ri in range(2) for m in range(4)], axis=0
        )
        turned.append(stacked.T)
    spin_x = turned[2] * t["ky"]
    spin_z = turned[1] * kappa_x - turned[0] * t["ky"]
    fields = turned + [spin_x, spin_z]
    even = jnp.concatenate([f[:64] for f in fields], axis=0)
    odd = jnp.concatenate([f[64:] for f in fields], axis=0)
    mixed = dot(even, t["first0"]) + dot(odd, t["first1"])
    upper, lower = [], []
    for n in range(5):
        plain = mixed[64 * n : 64 * n + 64, :128]
        times_i = mixed[64 * n : 64 * n + 64, 128:]
        if n >= 3:
            plain, times_i = times_i, -plain
        upper.append(plain * t["tyc"] + times_i * t["tys"])
        lower.append(times_i * t["tyc"] - plain * t["tys"])
    both = jnp.concatenate([jnp.concatenate(upper, axis=1), jnp.concatenate(lower, axis=1)], axis=0)
    blocks = dot(t["cs1"], both)
    return [blocks[:, 128 * n : 128 * n + 128] for n in range(5)]


def inverse_x(t, blocks):
    u, v, w, spin_x, spin_z = blocks
    six = [u, v, w, spin_x, w * t["kx"], spin_z]
    summed = dot(t["cs3"], jnp.concatenate(six, axis=1))
    rows = []
    for n in range(6):
        first = summed[:64, 128 * n : 128 * n + 128]
        second = summed[64:, 128 * n : 128 * n + 128]
        a = first * t["txc"] - second * t["txs"]
        b = first * t["txs"] + second * t["txc"]
        if n == 4:
            a, b = b, -a
        rows.append(jnp.concatenate([a, b], axis=1))
    fields = dot(jnp.concatenate(rows, axis=0), t["mixed"])
    return [fields[64 * n : 64 * n + 64] for n in range(6)]


def forward_x(t, fields):
    u, v, w, ox, oy, oz = fields
    left = lax.broadcasted_iota(jnp.int32, (64, 128), 1) < 64
    product_xy = jnp.where(left, v, w) * jnp.where(left, oz, ox) - jnp.where(left, w, u) * jnp.where(left, oy, oz)
    product_z = u * oy - v * ox
    mixed = [dot(product_xy, t["fx"]), dot(product_xy, t["fy"]), dot(product_z, t["fx"])]
    upper, lower = [], []
    for m in mixed:
        plain, times_i = m[:, :128], m[:, 128:]
        upper.append(plain * t["txc"] - times_i * t["txs"])
        lower.append(-(times_i * t["txc"] + plain * t["txs"]))
    both = jnp.concatenate([jnp.concatenate(upper, axis=1), jnp.concatenate(lower, axis=1)], axis=0)
    blocks = dot(t["cs4"], both)
    return [blocks[:, 128 * n : 128 * n + 128] for n in range(3)]


def forward_y(t, blocks):
    summed = dot(t["cs3"], jnp.concatenate(blocks, axis=1))
    rows = []
    for n in range(3):
        first = summed[:64, 128 * n : 128 * n + 128]
        second = summed[64:, 128 * n : 128 * n + 128]
        rows.append(
            jnp.concatenate(
                [first * t["tyc"] - second * t["tys"], first * t["tys"] + second * t["tyc"]], axis=1
            )
        )
    rows = jnp.concatenate(rows, axis=0)
    even, odd = dot(rows, t["last0"]), dot(rows, t["last1"])
    return [
        jnp.concatenate([even[64 * n : 64 * n + 64], odd[64 * n : 64 * n + 64]], axis=0).T for n in range(3)
    ]


def kernel(vh, sc, off, *rest):
    t = {name: rest[i] for i, name in enumerate(NAMES)}
    (vnew, snew, send1, recv1, send2, recv2, relay2, send3, recv3, relay3a, relay3b, send4, recv4,
     vsend, vrecv, vlo_s, vhi_s, vlo_r, vhi_r, sx, sy_s, sy_r, tile, side, coarse, fine,
     s1, r1, s2, r2, s3, r3, s4, r4, sv, rv, sm, rm) = rest[len(NAMES):]
    t = {name: ref[...] for name, ref in t.items()}

    g = lax.axis_index("group")
    r = lax.axis_index("row")
    c = lax.axis_index("col")
    w, z = c // 4, c % 4
    z_up, z_down, z_far = (z + 1) % 4, (z + 3) % 4, (z + 2) % 4
    up, down = (g, r, 4 * w + z_up), (g, r, 4 * w + z_down)
    c_next, c_prev = (g, r, (c + 1) % 64), (g, r, (c + 63) % 64)
    r_next, r_prev = (g, (r + 1) % 8, c), (g, (r + 7) % 8, c)
    plane_peers = [(g, r, 4 * ((w + d) % 16) + z) for d in range(1, 16)]
    row_peers = [(g, (r + d) % 8, c) for d in range(1, 8)]
    kept = jnp.logical_or(w < 6, w >= 10)

    barrier = pltpu.get_barrier_semaphore()
    greeted = plane_peers + row_peers + [up, down, c_next, c_prev]
    for peer in greeted:
        pl.semaphore_signal(barrier, inc=1, device_id=peer, device_id_type=MESH)

    def remote(src, dst, ssem, rsem, peer):
        return pltpu.make_async_remote_copy(
            src_ref=src, dst_ref=dst, send_sem=ssem, recv_sem=rsem, device_id=peer, device_id_type=MESH
        )

    def rows(ref, start, size):
        return ref.at[pl.ds(pl.multiple_of(start, 8), size), :]

    lane64 = lax.broadcasted_iota(jnp.int32, (1, 64), 1)
    wave = 8 * c + lane64 % 8
    kappa = jnp.where(wave < 256, wave, wave - 512).astype(jnp.float32) * (1.0 / 256.0)
    blocks = inverse_y(t, lambda comp, ri: vh[2 * comp + ri], kappa)
    zero = jnp.zeros((4, 128), jnp.float32)
    for d in range(16):
        part = [b[4 * d : 4 * d + 4] for b in blocks] + [zero]
        send1[24 * d : 24 * d + 24, :] = jnp.concatenate(part, axis=0)

    side[...] = jnp.zeros_like(side)
    coarse[...] = jnp.zeros_like(coarse)

    pl.semaphore_wait(barrier, len(greeted))

    sent1 = []
    for d in range(1, 16):
        to = (w + d) % 16
        copy = remote(rows(send1, 24 * to, 24), rows(recv1, 24 * w, 24), s1.at[d], r1.at[d], plane_peers[d - 1])
        copy.start()
        sent1.append(copy)
    tile_right = remote(sc, sx.at[0], sm.at[0], rm.at[0], r_next)
    tile_left = remote(sc, sx.at[1], sm.at[1], rm.at[1], r_prev)
    tile_right.start()
    tile_left.start()
    mine = pl.ds(pl.multiple_of(24 * w, 8), 24)
    recv1[mine, :] = send1[mine, :]
    for copy in sent1:
        copy.wait_recv()
    for k in range(4):
        for f in range(5):
            send2[k, 16 * f : 16 * f + 16, :] = recv1[pl.ds(4 * f + k, 16, stride=24), :]

    half = 40
    far_up = remote(send2.at[z_far, pl.ds(0, half)], relay2.at[0], s2.at[0], r2.at[0], up)
    far_down = remote(send2.at[z_far, pl.ds(half, half)], relay2.at[1], s2.at[1], r2.at[1], down)
    near_up = remote(send2.at[z_up], recv2.at[z], s2.at[2], r2.at[2], up)
    near_down = remote(send2.at[z_down], recv2.at[z], s2.at[3], r2.at[3], down)
    far_up.start()
    far_down.start()
    near_up.start()
    near_down.start()
    recv2[z] = send2[z]
    far_up.wait_recv()
    pass_up = remote(relay2.at[0], recv2.at[z_down, pl.ds(0, half)], s2.at[4], r2.at[4], up)
    pass_up.start()
    far_down.wait_recv()
    pass_down = remote(relay2.at[1], recv2.at[z_up, pl.ds(half, half)], s2.at[5], r2.at[5], down)
    pass_down.start()

    tile_right.wait_recv()
    tile_left.wait_recv()
    first_half = lax.broadcasted_iota(jnp.int32, (16, 128), 1) < 64
    for p in range(8):
        tile[24 * p + 4 : 24 * p + 20, :] = sc[p]
        side[24 * p + 4 : 24 * p + 20, :] = jnp.where(first_half, sx[1, p], sx[0, p])
    for i in range(4):
        sy_s[0, 8 * i : 8 * i + 8, :] = tile[pl.ds(16 + i, 8, stride=24), :]
        sy_s[1, 8 * i : 8 * i + 8, :] = tile[pl.ds(4 + i, 8, stride=24), :]
    for i in range(2):
        sy_s[0, 32 + 8 * i : 40 + 8 * i, :] = side[pl.ds(18 + i, 8, stride=24), :]
        sy_s[1, 32 + 8 * i : 40 + 8 * i, :] = side[pl.ds(4 + i, 8, stride=24), :]
    rim_next = remote(sy_s.at[0], sy_r.at[0], sm.at[2], rm.at[2], c_next)
    rim_prev = remote(sy_s.at[1], sy_r.at[1], sm.at[3], rm.at[3], c_prev)
    rim_next.start()
    rim_prev.start()

    near_up.wait_recv()
    near_down.wait_recv()
    pass_up.wait_recv()
    pass_down.wait_recv()

    landed = [
        jnp.concatenate([recv2[k, 16 * f : 16 * f + 16, :] for k in range(4)], axis=0) for f in range(5)
    ]
    fields = inverse_x(t, landed)
    leaving = forward_x(t, fields)
    for k in range(4):
        for f in range(3):
            send3[k, 12 * f : 12 * f + 12, :] = leaving[f][16 * k : 16 * k + 12]
        send3[k, 36:40, :] = zero
    far_up3 = remote(send3.at[z_far, pl.ds(0, 24)], relay3a, s3.at[0], r3.at[0], up)
    far_down3 = remote(send3.at[z_far, pl.ds(24, 16)], relay3b, s3.at[1], r3.at[1], down)
    near_up3 = remote(send3.at[z_up], rows(recv3, 40 * z, 40), s3.at[2], r3.at[2], up)
    near_down3 = remote(send3.at[z_down], rows(recv3, 40 * z, 40), s3.at[3], r3.at[3], down)
    far_up3.start()
    far_down3.start()
    near_up3.start()
    near_down3.start()
    recv3[pl.ds(pl.multiple_of(40 * z, 8), 40), :] = send3[z]

    left = lax.broadcasted_iota(jnp.int32, (64, 128), 1) < 64
    speeds = jnp.where(left, fields[0], fields[1]).T
    lines = []
    for f in range(2):
        lines.append(
            jnp.concatenate([speeds[64 * f + 8 * p : 64 * f + 8 * p + 8, :] for p in range(8)], axis=1)
        )
    lines = jnp.concatenate(lines, axis=0)
    rolled = pltpu.roll(lines, (513 - off[0]) % 512, 1)
    shifted = pltpu.roll(rolled, 448, 1)
    for k in range(4):
        vsend[2 * k] = rolled[:, 128 * k : 128 * k + 128]
        vsend[2 * k + 1] = shifted[:, 128 * k : 128 * k + 128]
    sentv = []
    for d in range(1, 8):
        copy = remote(vsend.at[(r + d) % 8], rows(vrecv, 16 * r, 16), sv.at[d], rv.at[d], row_peers[d - 1])
        copy.start()
        sentv.append(copy)
    vrecv[pl.ds(pl.multiple_of(16 * r, 8), 16), :] = vsend[r]

    far_up3.wait_recv()
    pass_up3 = remote(relay3a, rows(recv3, 40 * z_down, 24), s3.at[4], r3.at[4], up)
    pass_up3.start()
    far_down3.wait_recv()
    pass_down3 = remote(relay3b, rows(recv3, 40 * z_up + 24, 16), s3.at[5], r3.at[5], down)
    pass_down3.start()

    for copy in sentv:
        copy.wait_recv()
    for i, k in enumerate((0, 1, 8, 9)):
        vlo_s[8 * i : 8 * i + 8, :] = vrecv[pl.ds(k, 8, stride=16), :]
    for i, k in enumerate((7, 15)):
        vhi_s[8 * i : 8 * i + 8, :] = vrecv[pl.ds(k, 8, stride=16), :]
    low = remote(vlo_s, vlo_r, sm.at[4], rm.at[4], c_prev)
    high = remote(vhi_s, vhi_r, sm.at[5], rm.at[5], c_next)
    low.start()
    high.start()

    near_up3.wait_recv()
    near_down3.wait_recv()
    pass_up3.wait_recv()
    pass_down3.wait_recv()

    for k in range(12):
        part = [recv3[pl.ds(12 * f + k, 4, stride=40), :] for f in range(3)] + [zero]
        send4[k] = jnp.concatenate(part, axis=0)
    for d in range(1, 16):
        to = (w + d) % 16
        slot = jnp.where(to < 6, to, to - 4)

        @pl.when(jnp.logical_or(to < 6, to >= 10))
        def _():
            remote(send4.at[slot], rows(recv4, 16 * w, 16), s4.at[d], r4.at[d], plane_peers[d - 1]).start()

    @pl.when(kept)
    def _():
        recv4[pl.ds(pl.multiple_of(16 * w, 8), 16), :] = send4[jnp.where(w < 6, w, w - 4)]

    rim_next.wait_recv()
    rim_prev.wait_recv()
    for i in range(4):
        tile[pl.ds(i, 8, stride=24), :] = sy_r[0, 8 * i : 8 * i + 8, :]
        tile[pl.ds(20 + i, 8, stride=24), :] = sy_r[1, 8 * i : 8 * i + 8, :]
    for i in range(2):
        side[pl.ds(2 + i, 8, stride=24), :] = sy_r[0, 32 + 8 * i : 40 + 8 * i, :]
        side[pl.ds(20 + i, 8, stride=24), :] = sy_r[1, 32 + 8 * i : 40 + 8 * i, :]
    for p in range(8):
        coarse[24 * p : 24 * p + 16, :] = vrecv[16 * p : 16 * p + 16, :]
    low.wait_recv()
    high.wait_recv()
    for i in range(4):
        coarse[pl.ds(16 + i, 8, stride=24), :] = vlo_r[8 * i : 8 * i + 8, :]
    for i in range(2):
        coarse[pl.ds(20 + i, 8, stride=24), :] = vhi_r[8 * i : 8 * i + 8, :]
    fine[...] = dot(coarse[...], t["spread"])

    def one_plane(p, carry):
        block = pl.ds(pl.multiple_of(24 * p, 8), 24)
        speed = dot(t["lift"], fine[block, :])
        x_speed, y_speed = speed[:24], speed[24:]
        values = jnp.concatenate([tile[block, :], side[block, :]], axis=1)
        for _ in range(2):
            values = advance(values, x_speed, y_speed)
        snew[p] = values[4:20, :128]
        return carry

    lax.fori_loop(0, 8, one_plane, 0)

    row8 = 8 * c + lax.broadcasted_iota(jnp.int32, (8, 128), 0)
    wave_x = jnp.where(row8 < 256, row8, row8 - 512)
    squared_x = jnp.square(wave_x.astype(jnp.float32) * (1.0 / 256.0))
    damping, keep = [], []
    for m in range(4):
        column = 128 * m + lax.broadcasted_iota(jnp.int32, (8, 128), 1)
        wave_y = jnp.where(column < 256, column, column - 512)
        squared_y = jnp.square(wave_y.astype(jnp.float32) * (1.0 / 256.0))
        damping.append(jnp.exp(-viscosity * time_step * (squared_x + squared_y)))
        keep.append(jnp.logical_and(3 * jnp.abs(wave_x) < 512, 3 * jnp.abs(wave_y) < 512))

    @pl.when(jnp.logical_not(kept))
    def _():
        for n in range(6):
            for m in range(4):
                lanes = slice(128 * m, 128 * m + 128)
                vnew[n, :, lanes] = damping[m] * vh[n, :, lanes]

    @pl.when(kept)
    def _():
        for d in range(1, 16):
            remote(send4.at[0], rows(recv4, 0, 16), s4.at[d], r4.at[d], plane_peers[d - 1]).wait_recv()
        gathered = [
            jnp.concatenate([recv4[pl.ds(4 * f + k, 16, stride=16), :] for k in range(4)], axis=0)
            for f in range(3)
        ]
        forcing = forward_y(t, gathered)
        for f in range(3):
            for ri in range(2):
                for m in range(4):
                    lanes = slice(128 * m, 128 * m + 128)
                    push = forcing[f][32 * ri + 8 * m : 32 * ri + 8 * m + 8]
                    n = 2 * f + ri
                    vnew[n, :, lanes] = damping[m] * (
                        vh[n, :, lanes] + time_step * jnp.where(keep[m], push, 0.0)
                    )

    for copy in sent1 + sentv + [
        tile_right, tile_left, far_up, far_down, near_up, near_down, pass_up, pass_down, rim_next, rim_prev,
        far_up3, far_down3, near_up3, near_down3, pass_up3, pass_down3, low, high,
    ]:
        copy.wait_send()
    for d in range(1, 16):
        to = (w + d) % 16

        @pl.when(jnp.logical_or(to < 6, to >= 10))
        def _():
            remote(send4.at[0], rows(recv4, 0, 16), s4.at[d], r4.at[d], plane_peers[d - 1]).wait_send()


def advance(values, x_speed, y_speed):
    height, breadth = values.shape

    def along(axis, step):
        return pltpu.roll(values, (-step) % values.shape[axis], axis)

    def parts(axis):
        two_back, back, ahead, two_ahead = (along(axis, s) for s in (-2, -1, 1, 2))
        grad = (two_back - two_ahead + 8.0 * (ahead - back)) * (1.0 / 12.0)
        lap = (16.0 * (ahead + back) - two_ahead - two_back - 30.0 * values) * (1.0 / 12.0)
        return grad, lap

    grad_x, lap_x = parts(1)
    grad_y, lap_y = parts(0)
    return values + substep * (diffusivity * (lap_x + lap_y) - (x_speed * grad_x + y_speed * grad_y))


def per_device(velocity_hat, scalar, tile_offset):
    consts = tables()
    f32 = jnp.float32
    vmem = pl.BlockSpec(memory_space=pltpu.VMEM)
    dma = pltpu.SemaphoreType.DMA

    def buf(*shape):
        return pltpu.VMEM(shape, f32)

    vnew, snew = pl.pallas_call(
        kernel,
        name="coupled_step",
        out_shape=(jax.ShapeDtypeStruct((6, 8, 512), f32), jax.ShapeDtypeStruct((8, 16, 128), f32)),
        in_specs=[vmem, vmem, pl.BlockSpec(memory_space=pltpu.SMEM)] + [vmem] * len(NAMES),
        out_specs=(vmem, vmem),
        scratch_shapes=[
            buf(384, 128), buf(384, 128), buf(4, 80, 128), buf(4, 80, 128), buf(2, 40, 128),
            buf(4, 40, 128), buf(160, 128), buf(24, 128), buf(16, 128), buf(12, 16, 128), buf(256, 128),
            buf(8, 16, 128), buf(128, 128), buf(32, 128), buf(16, 128), buf(32, 128), buf(16, 128),
            buf(2, 8, 16, 128), buf(2, 48, 128), buf(2, 48, 128), buf(192, 128), buf(192, 128),
            buf(192, 128), buf(192, 256),
            dma((16,)), dma((16,)), dma((6,)), dma((6,)), dma((6,)), dma((6,)), dma((16,)), dma((16,)),
            dma((8,)), dma((8,)), dma((6,)), dma((6,)),
        ],
        compiler_params=pltpu.CompilerParams(collective_id=0, has_side_effects=True),
    )(velocity_hat.reshape(6, 8, 512), scalar, tile_offset, *[jnp.asarray(consts[k]) for k in NAMES])
    return vnew.reshape(3, 2, 1, 8, 512), snew


def solution(mesh):
    return jax.shard_map(
        per_device,
        mesh=mesh,
        in_specs=(P(None, None, ("group", "row"), "col", None), P("group", "col", "row"), P()),
        out_specs=(P(None, None, ("group", "row"), "col", None), P("group", "col", "row")),
        check_vma=False,
    )
```

profile of v0, /device:TPU:32, one launch (start us, length us, event | category | flops | bytes accessed | tf_op | source)
XLA Modules:
  0.0 87.7 jit_solution(4010632049986235502)
XLA Ops:
  1.3 84.2 %coupled_step.1 = (f32[6,8,512]{2,1,0:T(8,128)}, f32[8,16,128]{2,1,0:T(8,128)}) custom-call(f32[6,8,512]{2,1,0:T(8,128)} %bitcast.5, f32[8,16,128]{2,1,0:T(8,128)} %sc.1, s32[1]{0:T(128)S(6)} %copy.26.off, f32[64,256]{1,0:T(8,128)} %constant.36.clone.rest_0_, f32[64,256]{1,0:T(8,128)} %constant.37.clone.rest_1_, f32[64,128]{1,0:T(8,128)} %constant.38.clone.rest_2_, ...), custom_call_target="tpu_custom_call" | custom-call | tf_op jit(solution)/shard_map/coupled_step/pallas_call | solution.py:505
  85.5 0.0 copy-start
  85.5 1.6 %copy.27 = f32[3,2,1,8,512]{4,3,2,1,0:T(8,128)} copy(f32[3,2,1,8,512]{4,3,2,1,0:T(8,128)} %bitcast.4) | data formatting | bytes 196608
  87.0 0.0 copy-done
  87.0 0.6 copy.28
Async XLA Ops:
  85.5 1.6 %copy-start = (f32[8,16,128]{2,1,0:T(8,128)S(1)}, f32[8,16,128]{2,1,0:T(8,128)}, u32[]{:S(2)}) copy-start(f32[8,16,128]{2,1,0:T(8,128)} %get-tuple-element.11) | copy-start | bytes 196612
where the time goes:
time: 87.9 us; the launch traced here: 87.7 us
  Pallas kernels  84.2 us (96%)
  local copies, waits for them, and re-layouts  2.2 us (3%)
  between operations  1.29 us (1%)
    pallas_call x1, Pallas kernels, per_device(): pl.pallas_call(kernel, name='coupled_step', out_shape=(jax.ShapeDtypeStru...  84.2 us
    unnamed x4, local copies, waits for them, and re-layouts  2.2 us

commit v1 on v0

--- a/solution.py
+++ b/solution.py
@@ -218,8 +218,8 @@
 
 def kernel(vh, sc, off, *rest):
     t = {name: rest[i] for i, name in enumerate(NAMES)}
-    (vnew, snew, send1, recv1, send2, recv2, relay2, send3, recv3, relay3a, relay3b, send4, recv4,
-     vsend, vrecv, vlo_s, vhi_s, vlo_r, vhi_r, sx, sy_s, sy_r, tile, side, coarse, fine,
+    (vnew, snew, send1, recv1, send2, recv2, relay2, send3, recv3, send4, recv4,
+     vsend, vrecv, vlo_s, vhi_s, vlo_r, vhi_r, edge_s, edge_r, rim_s, rim_r, corner_s, corner_r, turned, tile, side, coarse, fine,
      s1, r1, s2, r2, s3, r3, s4, r4, sv, rv, sm, rm) = rest[len(NAMES):]
     t = {name: ref[...] for name, ref in t.items()}
 
@@ -228,7 +228,7 @@
     c = lax.axis_index("col")
     w, z = c // 4, c % 4
     z_up, z_down, z_far = (z + 1) % 4, (z + 3) % 4, (z + 2) % 4
-    up, down = (g, r, 4 * w + z_up), (g, r, 4 * w + z_down)
+    up, down, opposite = (g, r, 4 * w + z_up), (g, r, 4 * w + z_down), (g, r, 4 * w + z_far)
     c_next, c_prev = (g, r, (c + 1) % 64), (g, r, (c + 63) % 64)
     r_next, r_prev = (g, (r + 1) % 8, c), (g, (r + 7) % 8, c)
     plane_peers = [(g, r, 4 * ((w + d) % 16) + z) for d in range(1, 16)]
@@ -259,19 +259,32 @@
 
     side[...] = jnp.zeros_like(side)
     coarse[...] = jnp.zeros_like(coarse)
+    for p in range(8):
+        turned[16 * p : 16 * p + 16, :] = sc[p]
+        tile[24 * p + 4 : 24 * p + 20, :] = sc[p]
+    flat = turned[...].T
+    edge_s[0] = flat[120:128]
+    edge_s[1] = flat[0:8]
+    for i in range(4):
+        rim_s[0, 8 * i : 8 * i + 8, :] = turned[pl.ds(12 + i, 8, stride=16), :]
+        rim_s[1, 8 * i : 8 * i + 8, :] = turned[pl.ds(i, 8, stride=16), :]
 
     pl.semaphore_wait(barrier, len(greeted))
 
+    edge_right = remote(edge_s.at[0], edge_r.at[0], sm.at[0], rm.at[0], r_next)
+    edge_left = remote(edge_s.at[1], edge_r.at[1], sm.at[1], rm.at[1], r_prev)
+    rim_next = remote(rim_s.at[0], rim_r.at[0], sm.at[2], rm.at[2], c_next)
+    rim_prev = remote(rim_s.at[1], rim_r.at[1], sm.at[3], rm.at[3], c_prev)
+    edge_right.start()
+    edge_left.start()
     sent1 = []
     for d in range(1, 16):
         to = (w + d) % 16
         copy = remote(rows(send1, 24 * to, 24), rows(recv1, 24 * w, 24), s1.at[d], r1.at[d], plane_peers[d - 1])
         copy.start()
         sent1.append(copy)
-    tile_right = remote(sc, sx.at[0], sm.at[0], rm.at[0], r_next)
-    tile_left = remote(sc, sx.at[1], sm.at[1], rm.at[1], r_prev)
-    tile_right.start()
-    tile_left.start()
+    rim_next.start()
+    rim_prev.start()
     mine = pl.ds(pl.multiple_of(24 * w, 8), 24)
     recv1[mine, :] = send1[mine, :]
     for copy in sent1:
@@ -297,22 +310,18 @@
     pass_down = remote(relay2.at[1], recv2.at[z_up, pl.ds(half, half)], s2.at[5], r2.at[5], down)
     pass_down.start()
 
-    tile_right.wait_recv()
-    tile_left.wait_recv()
-    first_half = lax.broadcasted_iota(jnp.int32, (16, 128), 1) < 64
+    edge_right.wait_recv()
+    edge_left.wait_recv()
+    corner_s[...] = jnp.concatenate(
+        [edge_r[1, 0:2, :], edge_r[0, 6:8, :], jnp.zeros((4, 128), jnp.float32)], axis=0
+    )
+    corner_next = remote(corner_s, corner_r.at[0], sm.at[6], rm.at[6], c_next)
+    corner_prev = remote(corner_s, corner_r.at[1], sm.at[7], rm.at[7], c_prev)
+    corner_next.start()
+    corner_prev.start()
+    beside = jnp.concatenate([edge_r[1], jnp.zeros((112, 128), jnp.float32), edge_r[0]], axis=0).T
     for p in range(8):
-        tile[24 * p + 4 : 24 * p + 20, :] = sc[p]
-        side[24 * p + 4 : 24 * p + 20, :] = jnp.where(first_half, sx[1, p], sx[0, p])
-    for i in range(4):
-        sy_s[0, 8 * i : 8 * i + 8, :] = tile[pl.ds(16 + i, 8, stride=24), :]
-        sy_s[1, 8 * i : 8 * i + 8, :] = tile[pl.ds(4 + i, 8, stride=24), :]
-    for i in range(2):
-        sy_s[0, 32 + 8 * i : 40 + 8 * i, :] = side[pl.ds(18 + i, 8, stride=24), :]
-        sy_s[1, 32 + 8 * i : 40 + 8 * i, :] = side[pl.ds(4 + i, 8, stride=24), :]
-    rim_next = remote(sy_s.at[0], sy_r.at[0], sm.at[2], rm.at[2], c_next)
-    rim_prev = remote(sy_s.at[1], sy_r.at[1], sm.at[3], rm.at[3], c_prev)
-    rim_next.start()
-    rim_prev.start()
+        side[24 * p + 4 : 24 * p + 20, :] = beside[16 * p : 16 * p + 16]
 
     near_up.wait_recv()
     near_down.wait_recv()
@@ -328,14 +337,21 @@
         for f in range(3):
             send3[k, 12 * f : 12 * f + 12, :] = leaving[f][16 * k : 16 * k + 12]
         send3[k, 36:40, :] = zero
-    far_up3 = remote(send3.at[z_far, pl.ds(0, 24)], relay3a, s3.at[0], r3.at[0], up)
-    far_down3 = remote(send3.at[z_far, pl.ds(24, 16)], relay3b, s3.at[1], r3.at[1], down)
-    near_up3 = remote(send3.at[z_up], rows(recv3, 40 * z, 40), s3.at[2], r3.at[2], up)
-    near_down3 = remote(send3.at[z_down], rows(recv3, 40 * z, 40), s3.at[3], r3.at[3], down)
-    far_up3.start()
-    far_down3.start()
+    far3 = remote(send3.at[z_far], rows(recv3, 40 * z, 40), s3.at[0], r3.at[0], opposite)
+    near_up3 = remote(send3.at[z_up], rows(recv3, 40 * z, 40), s3.at[1], r3.at[1], up)
+    near_down3 = remote(send3.at[z_down], rows(recv3, 40 * z, 40), s3.at[2], r3.at[2], down)
+
+    @pl.when(z % 2 == 0)
+    def _():
+        far3.start()
+
     near_up3.start()
     near_down3.start()
+
+    @pl.when(z % 2 == 1)
+    def _():
+        far3.start()
+
     recv3[pl.ds(pl.multiple_of(40 * z, 8), 40), :] = send3[z]
 
     left = lax.broadcasted_iota(jnp.int32, (64, 128), 1) < 64
@@ -358,13 +374,6 @@
         sentv.append(copy)
     vrecv[pl.ds(pl.multiple_of(16 * r, 8), 16), :] = vsend[r]
 
-    far_up3.wait_recv()
-    pass_up3 = remote(relay3a, rows(recv3, 40 * z_down, 24), s3.at[4], r3.at[4], up)
-    pass_up3.start()
-    far_down3.wait_recv()
-    pass_down3 = remote(relay3b, rows(recv3, 40 * z_up + 24, 16), s3.at[5], r3.at[5], down)
-    pass_down3.start()
-
     for copy in sentv:
         copy.wait_recv()
     for i, k in enumerate((0, 1, 8, 9)):
@@ -378,8 +387,7 @@
 
     near_up3.wait_recv()
     near_down3.wait_recv()
-    pass_up3.wait_recv()
-    pass_down3.wait_recv()
+    far3.wait_recv()
 
     for k in range(12):
         part = [recv3[pl.ds(12 * f + k, 4, stride=40), :] for f in range(3)] + [zero]
@@ -399,11 +407,16 @@
     rim_next.wait_recv()
     rim_prev.wait_recv()
     for i in range(4):
-        tile[pl.ds(i, 8, stride=24), :] = sy_r[0, 8 * i : 8 * i + 8, :]
-        tile[pl.ds(20 + i, 8, stride=24), :] = sy_r[1, 8 * i : 8 * i + 8, :]
-    for i in range(2):
-        side[pl.ds(2 + i, 8, stride=24), :] = sy_r[0, 32 + 8 * i : 40 + 8 * i, :]
-        side[pl.ds(20 + i, 8, stride=24), :] = sy_r[1, 32 + 8 * i : 40 + 8 * i, :]
+        tile[pl.ds(i, 8, stride=24), :] = rim_r[0, 8 * i : 8 * i + 8, :]
+        tile[pl.ds(20 + i, 8, stride=24), :] = rim_r[1, 8 * i : 8 * i + 8, :]
+    corner_next.wait_recv()
+    corner_prev.wait_recv()
+    for n in range(2):
+        turned[...] = jnp.concatenate(
+            [corner_r[n, 0:2, :], jnp.zeros((124, 128), jnp.float32), corner_r[n, 2:4, :]], axis=0
+        ).T
+        for i in range(2):
+            side[pl.ds(2 + 18 * n + i, 8, stride=24), :] = turned[pl.ds(14 * (1 - n) + i, 8, stride=16), :]
     for p in range(8):
         coarse[24 * p : 24 * p + 16, :] = vrecv[16 * p : 16 * p + 16, :]
     low.wait_recv()
@@ -464,8 +477,8 @@
                     )
 
     for copy in sent1 + sentv + [
-        tile_right, tile_left, far_up, far_down, near_up, near_down, pass_up, pass_down, rim_next, rim_prev,
-        far_up3, far_down3, near_up3, near_down3, pass_up3, pass_down3, low, high,
+        edge_right, edge_left, rim_next, rim_prev, corner_next, corner_prev, far_up, far_down, near_up, near_down,
+        pass_up, pass_down, far3, near_up3, near_down3, low, high,
     ]:
         copy.wait_send()
     for d in range(1, 16):
@@ -510,12 +523,13 @@
         out_specs=(vmem, vmem),
         scratch_shapes=[
             buf(384, 128), buf(384, 128), buf(4, 80, 128), buf(4, 80, 128), buf(2, 40, 128),
-            buf(4, 40, 128), buf(160, 128), buf(24, 128), buf(16, 128), buf(12, 16, 128), buf(256, 128),
+            buf(4, 40, 128), buf(160, 128), buf(12, 16, 128), buf(256, 128),
             buf(8, 16, 128), buf(128, 128), buf(32, 128), buf(16, 128), buf(32, 128), buf(16, 128),
-            buf(2, 8, 16, 128), buf(2, 48, 128), buf(2, 48, 128), buf(192, 128), buf(192, 128),
+            buf(2, 8, 128), buf(2, 8, 128), buf(2, 32, 128), buf(2, 32, 128), buf(8, 128), buf(2, 8, 128), buf(128, 128),
+            buf(192, 128), buf(192, 128),
             buf(192, 128), buf(192, 256),
-            dma((16,)), dma((16,)), dma((6,)), dma((6,)), dma((6,)), dma((6,)), dma((16,)), dma((16,)),
-            dma((8,)), dma((8,)), dma((6,)), dma((6,)),
+            dma((16,)), dma((16,)), dma((6,)), dma((6,)), dma((3,)), dma((3,)), dma((16,)), dma((16,)),
+            dma((8,)), dma((8,)), dma((8,)), dma((8,)),
         ],
         compiler_params=pltpu.CompilerParams(collective_id=0, has_side_effects=True),
     )(velocity_hat.reshape(6, 8, 512), scalar, tile_offset, *[jnp.asarray(consts[k]) for k in NAMES])

time: 87.9 us -> 82.1 us (0.934)
  the two profiles are of different devices: /device:TPU:32 before, /device:TPU:16 now
where the time goes in v1:
time: 82.1 us; the launch traced here: 81.9 us
  Pallas kernels  78.4 us (95%)
  local copies, waits for them, and re-layouts  2.2 us (3%)
  between operations  1.29 us (2%)
    pallas_call x1, Pallas kernels, per_device(): pl.pallas_call(kernel, name='coupled_step', out_shape=(jax.ShapeDtypeStru...  78.4 us
    unnamed x4, local copies, waits for them, and re-layouts  2.2 us

profile of v1, /device:TPU:16, one launch (start us, length us, event | category | flops | bytes accessed | tf_op | source)
XLA Modules:
  0.0 81.9 jit_solution(3574005655559819626)
XLA Ops:
  1.3 78.4 %coupled_step.1 = (f32[6,8,512]{2,1,0:T(8,128)}, f32[8,16,128]{2,1,0:T(8,128)}) custom-call(f32[6,8,512]{2,1,0:T(8,128)} %bitcast.5, f32[8,16,128]{2,1,0:T(8,128)} %sc.1, s32[1]{0:T(128)S(6)} %copy.26.off, f32[64,256]{1,0:T(8,128)} %constant.36.clone.rest_0_, f32[64,256]{1,0:T(8,128)} %constant.37.clone.rest_1_, f32[64,128]{1,0:T(8,128)} %constant.38.clone.rest_2_, ...), custom_call_target="tpu_custom_call" | custom-call | tf_op jit(solution)/shard_map/coupled_step/pallas_call | solution.py:518
  79.7 0.0 copy-start
  79.7 1.6 %copy.27 = f32[3,2,1,8,512]{4,3,2,1,0:T(8,128)} copy(f32[3,2,1,8,512]{4,3,2,1,0:T(8,128)} %bitcast.4) | data formatting | bytes 196608
  81.3 0.0 copy-done
  81.3 0.6 copy.28
Async XLA Ops:
  79.7 1.6 %copy-start = (f32[8,16,128]{2,1,0:T(8,128)S(1)}, f32[8,16,128]{2,1,0:T(8,128)}, u32[]{:S(2)}) copy-start(f32[8,16,128]{2,1,0:T(8,128)} %get-tuple-element.11) | copy-start | bytes 196612

commit v2 on v1

--- a/solution.py
+++ b/solution.py
@@ -220,7 +220,7 @@
     t = {name: rest[i] for i, name in enumerate(NAMES)}
     (vnew, snew, send1, recv1, send2, recv2, relay2, send3, recv3, send4, recv4,
      vsend, vrecv, vlo_s, vhi_s, vlo_r, vhi_r, edge_s, edge_r, rim_s, rim_r, corner_s, corner_r, turned, tile, side, coarse, fine,
-     s1, r1, s2, r2, s3, r3, s4, r4, sv, rv, sm, rm) = rest[len(NAMES):]
+     s1, r1, s2, r2, s3, r3, s4, r4, sv, rv, sl, rl, sh, rh, sm, rm, row_sem) = rest[len(NAMES):]
     t = {name: ref[...] for name, ref in t.items()}
 
     g = lax.axis_index("group")
@@ -270,6 +270,8 @@
         rim_s[1, 8 * i : 8 * i + 8, :] = turned[pl.ds(i, 8, stride=16), :]
 
     pl.semaphore_wait(barrier, len(greeted))
+    for peer in row_peers:
+        pl.semaphore_signal(row_sem, inc=1, device_id=peer, device_id_type=MESH)
 
     edge_right = remote(edge_s.at[0], edge_r.at[0], sm.at[0], rm.at[0], r_next)
     edge_left = remote(edge_s.at[1], edge_r.at[1], sm.at[1], rm.at[1], r_prev)
@@ -280,7 +282,7 @@
     sent1 = []
     for d in range(1, 16):
         to = (w + d) % 16
-        copy = remote(rows(send1, 24 * to, 24), rows(recv1, 24 * w, 24), s1.at[d], r1.at[d], plane_peers[d - 1])
+        copy = remote(rows(send1, 24 * to, 20), rows(recv1, 24 * w, 20), s1.at[d], r1.at[d], plane_peers[d - 1])
         copy.start()
         sent1.append(copy)
     rim_next.start()
@@ -337,9 +339,10 @@
         for f in range(3):
             send3[k, 12 * f : 12 * f + 12, :] = leaving[f][16 * k : 16 * k + 12]
         send3[k, 36:40, :] = zero
-    far3 = remote(send3.at[z_far], rows(recv3, 40 * z, 40), s3.at[0], r3.at[0], opposite)
-    near_up3 = remote(send3.at[z_up], rows(recv3, 40 * z, 40), s3.at[1], r3.at[1], up)
-    near_down3 = remote(send3.at[z_down], rows(recv3, 40 * z, 40), s3.at[2], r3.at[2], down)
+    kept_rows = pl.ds(0, 36)
+    far3 = remote(send3.at[z_far, kept_rows], rows(recv3, 40 * z, 36), s3.at[0], r3.at[0], opposite)
+    near_up3 = remote(send3.at[z_up, kept_rows], rows(recv3, 40 * z, 36), s3.at[1], r3.at[1], up)
+    near_down3 = remote(send3.at[z_down, kept_rows], rows(recv3, 40 * z, 36), s3.at[2], r3.at[2], down)
 
     @pl.when(z % 2 == 0)
     def _():
@@ -367,23 +370,25 @@
     for k in range(4):
         vsend[2 * k] = rolled[:, 128 * k : 128 * k + 128]
         vsend[2 * k + 1] = shifted[:, 128 * k : 128 * k + 128]
+        for n, source in enumerate((rolled, shifted)):
+            part = source[:, 128 * k : 128 * k + 128]
+            vlo_s[2 * k + n] = jnp.concatenate([part[0:2], part[8:10], zero], axis=0)
+            vhi_s[2 * k + n] = jnp.concatenate([part[7:8], part[15:16], zero, zero[:2]], axis=0)
+    pl.semaphore_wait(row_sem, 7)
     sentv = []
     for d in range(1, 8):
         copy = remote(vsend.at[(r + d) % 8], rows(vrecv, 16 * r, 16), sv.at[d], rv.at[d], row_peers[d - 1])
         copy.start()
         sentv.append(copy)
+    sentr = []
+    for d in range(8):
+        to = (r + d) % 8
+        low = remote(vlo_s.at[to, pl.ds(0, 4)], vlo_r.at[r, pl.ds(0, 4)], sl.at[d], rl.at[d], (g, to, (c + 63) % 64))
+        high = remote(vhi_s.at[to, pl.ds(0, 2)], vhi_r.at[r, pl.ds(0, 2)], sh.at[d], rh.at[d], (g, to, (c + 1) % 64))
+        low.start()
+        high.start()
+        sentr += [low, high]
     vrecv[pl.ds(pl.multiple_of(16 * r, 8), 16), :] = vsend[r]
-
-    for copy in sentv:
-        copy.wait_recv()
-    for i, k in enumerate((0, 1, 8, 9)):
-        vlo_s[8 * i : 8 * i + 8, :] = vrecv[pl.ds(k, 8, stride=16), :]
-    for i, k in enumerate((7, 15)):
-        vhi_s[8 * i : 8 * i + 8, :] = vrecv[pl.ds(k, 8, stride=16), :]
-    low = remote(vlo_s, vlo_r, sm.at[4], rm.at[4], c_prev)
-    high = remote(vhi_s, vhi_r, sm.at[5], rm.at[5], c_next)
-    low.start()
-    high.start()
 
     near_up3.wait_recv()
     near_down3.wait_recv()
@@ -417,14 +422,12 @@
         ).T
         for i in range(2):
             side[pl.ds(2 + 18 * n + i, 8, stride=24), :] = turned[pl.ds(14 * (1 - n) + i, 8, stride=16), :]
+    for copy in sentv + sentr:
+        copy.wait_recv()
     for p in range(8):
         coarse[24 * p : 24 * p + 16, :] = vrecv[16 * p : 16 * p + 16, :]
-    low.wait_recv()
-    high.wait_recv()
-    for i in range(4):
-        coarse[pl.ds(16 + i, 8, stride=24), :] = vlo_r[8 * i : 8 * i + 8, :]
-    for i in range(2):
-        coarse[pl.ds(20 + i, 8, stride=24), :] = vhi_r[8 * i : 8 * i + 8, :]
+        coarse[24 * p + 16 : 24 * p + 20, :] = vlo_r[p, 0:4, :]
+        coarse[24 * p + 20 : 24 * p + 22, :] = vhi_r[p, 0:2, :]
     fine[...] = dot(coarse[...], t["spread"])
 
     def one_plane(p, carry):
@@ -478,8 +481,8 @@
 
     for copy in sent1 + sentv + [
         edge_right, edge_left, rim_next, rim_prev, corner_next, corner_prev, far_up, far_down, near_up, near_down,
-        pass_up, pass_down, far3, near_up3, near_down3, low, high,
-    ]:
+        pass_up, pass_down, far3, near_up3, near_down3,
+    ] + sentr:
         copy.wait_send()
     for d in range(1, 16):
         to = (w + d) % 16
@@ -524,12 +527,13 @@
         scratch_shapes=[
             buf(384, 128), buf(384, 128), buf(4, 80, 128), buf(4, 80, 128), buf(2, 40, 128),
             buf(4, 40, 128), buf(160, 128), buf(12, 16, 128), buf(256, 128),
-            buf(8, 16, 128), buf(128, 128), buf(32, 128), buf(16, 128), buf(32, 128), buf(16, 128),
+            buf(8, 16, 128), buf(128, 128), buf(8, 8, 128), buf(8, 8, 128), buf(8, 8, 128), buf(8, 8, 128),
             buf(2, 8, 128), buf(2, 8, 128), buf(2, 32, 128), buf(2, 32, 128), buf(8, 128), buf(2, 8, 128), buf(128, 128),
             buf(192, 128), buf(192, 128),
             buf(192, 128), buf(192, 256),
             dma((16,)), dma((16,)), dma((6,)), dma((6,)), dma((3,)), dma((3,)), dma((16,)), dma((16,)),
-            dma((8,)), dma((8,)), dma((8,)), dma((8,)),
+            dma((8,)), dma((8,)), dma((8,)), dma((8,)), dma((8,)), dma((8,)), dma((8,)), dma((8,)),
+            pltpu.SemaphoreType.REGULAR,
         ],
         compiler_params=pltpu.CompilerParams(collective_id=0, has_side_effects=True),
     )(velocity_hat.reshape(6, 8, 512), scalar, tile_offset, *[jnp.asarray(consts[k]) for k in NAMES])

time: 82.1 us -> 79.4 us (0.967)
  the two profiles are of different devices: /device:TPU:16 before, /device:TPU:10 now
where the time goes in v2:
time: 79.4 us; the launch traced here: 79.2 us
  Pallas kernels  75.7 us (95%)
  local copies, waits for them, and re-layouts  2.2 us (3%)
  between operations  1.29 us (2%)
    pallas_call x1, Pallas kernels, per_device(): pl.pallas_call(kernel, name='coupled_step', out_shape=(jax.ShapeDtypeStru...  75.7 us
    unnamed x4, local copies, waits for them, and re-layouts  2.2 us

profile of v2, /device:TPU:10, one launch (start us, length us, event | category | flops | bytes accessed | tf_op | source)
XLA Modules:
  0.0 79.2 jit_solution(7718013880155827685)
XLA Ops:
  1.3 75.7 %coupled_step.1 = (f32[6,8,512]{2,1,0:T(8,128)}, f32[8,16,128]{2,1,0:T(8,128)}) custom-call(f32[6,8,512]{2,1,0:T(8,128)} %bitcast.5, f32[8,16,128]{2,1,0:T(8,128)} %sc.1, s32[1]{0:T(128)S(6)} %copy.26.off, f32[64,256]{1,0:T(8,128)} %constant.36.clone.rest_0_, f32[64,256]{1,0:T(8,128)} %constant.37.clone.rest_1_, f32[64,128]{1,0:T(8,128)} %constant.38.clone.rest_2_, ...), custom_call_target="tpu_custom_call" | custom-call | tf_op jit(solution)/shard_map/coupled_step/pallas_call | solution.py:521
  77.0 0.0 copy-start
  77.0 1.6 %copy.27 = f32[3,2,1,8,512]{4,3,2,1,0:T(8,128)} copy(f32[3,2,1,8,512]{4,3,2,1,0:T(8,128)} %bitcast.4) | data formatting | bytes 196608
  78.5 0.0 copy-done
  78.6 0.6 copy.28
Async XLA Ops:
  77.0 1.6 %copy-start = (f32[8,16,128]{2,1,0:T(8,128)S(1)}, f32[8,16,128]{2,1,0:T(8,128)}, u32[]{:S(2)}) copy-start(f32[8,16,128]{2,1,0:T(8,128)} %get-tuple-element.11) | copy-start | bytes 196612

commit v3 on v2

--- a/solution.py
+++ b/solution.py
@@ -135,8 +135,18 @@
          "last0", "last1", "ky", "kx", "spread", "lift"]
 
 
+def split(a):
+    high = a.astype(jnp.bfloat16)
+    return high, (a - high.astype(jnp.float32)).astype(jnp.bfloat16)
+
+
 def dot(a, b):
-    return jnp.dot(a, b, precision=lax.Precision.HIGHEST, preferred_element_type=jnp.float32)
+    (a_high, a_low), (b_high, b_low) = split(a), split(b)
+
+    def product(x, y):
+        return jnp.dot(x, y, preferred_element_type=jnp.float32)
+
+    return product(a_high, b_high) + (product(a_high, b_low) + product(a_low, b_high))
 
 
 def inverse_y(t, spectra, kappa_x):
@@ -216,12 +226,13 @@
     ]
 
 
-def kernel(vh, sc, off, *rest):
-    t = {name: rest[i] for i, name in enumerate(NAMES)}
+def kernel(vh_far, sc_far, off, *rest):
+    n_tables = len(NAMES)
+    far_tables, near_tables = rest[:n_tables], rest[-n_tables:]
+    rest = rest[:-n_tables]
     (vnew, snew, send1, recv1, send2, recv2, relay2, send3, recv3, send4, recv4,
      vsend, vrecv, vlo_s, vhi_s, vlo_r, vhi_r, edge_s, edge_r, rim_s, rim_r, corner_s, corner_r, turned, tile, side, coarse, fine,
-     s1, r1, s2, r2, s3, r3, s4, r4, sv, rv, sl, rl, sh, rh, sm, rm, row_sem) = rest[len(NAMES):]
-    t = {name: ref[...] for name, ref in t.items()}
+     s1, r1, s2, r2, s3, r3, s4, r4, sv, rv, sl, rl, sh, rh, sm, rm, row_sem, vh, sc, load) = rest[n_tables:]
 
     g = lax.axis_index("group")
     r = lax.axis_index("row")
@@ -239,6 +250,15 @@
     greeted = plane_peers + row_peers + [up, down, c_next, c_prev]
     for peer in greeted:
         pl.semaphore_signal(barrier, inc=1, device_id=peer, device_id_type=MESH)
+
+    fetched = [pltpu.make_async_copy(vh_far, vh, load.at[0]), pltpu.make_async_copy(sc_far, sc, load.at[1])]
+    for n in range(n_tables):
+        fetched.append(pltpu.make_async_copy(far_tables[n], near_tables[n], load.at[2 + n]))
+    for copy in fetched:
+        copy.start()
+    for copy in fetched:
+        copy.wait()
+    t = {name: near_tables[n][...] for n, name in enumerate(NAMES)}
 
     def remote(src, dst, ssem, rsem, peer):
         return pltpu.make_async_remote_copy(
@@ -513,6 +533,7 @@
     consts = tables()
     f32 = jnp.float32
     vmem = pl.BlockSpec(memory_space=pltpu.VMEM)
+    far = pl.BlockSpec(memory_space=pl.ANY)
     dma = pltpu.SemaphoreType.DMA
 
     def buf(*shape):
@@ -522,7 +543,7 @@
         kernel,
         name="coupled_step",
         out_shape=(jax.ShapeDtypeStruct((6, 8, 512), f32), jax.ShapeDtypeStruct((8, 16, 128), f32)),
-        in_specs=[vmem, vmem, pl.BlockSpec(memory_space=pltpu.SMEM)] + [vmem] * len(NAMES),
+        in_specs=[far, far, pl.BlockSpec(memory_space=pltpu.SMEM)] + [far] * len(NAMES),
         out_specs=(vmem, vmem),
         scratch_shapes=[
             buf(384, 128), buf(384, 128), buf(4, 80, 128), buf(4, 80, 128), buf(2, 40, 128),
@@ -533,8 +554,8 @@
             buf(192, 128), buf(192, 256),
             dma((16,)), dma((16,)), dma((6,)), dma((6,)), dma((3,)), dma((3,)), dma((16,)), dma((16,)),
             dma((8,)), dma((8,)), dma((8,)), dma((8,)), dma((8,)), dma((8,)), dma((8,)), dma((8,)),
-            pltpu.SemaphoreType.REGULAR,
-        ],
+            pltpu.SemaphoreType.REGULAR, buf(6, 8, 512), buf(8, 16, 128), dma((2 + len(NAMES),)),
+        ] + [buf(*consts[k].shape) for k in NAMES],
         compiler_params=pltpu.CompilerParams(collective_id=0, has_side_effects=True),
     )(velocity_hat.reshape(6, 8, 512), scalar, tile_offset, *[jnp.asarray(consts[k]) for k in NAMES])
     return vnew.reshape(3, 2, 1, 8, 512), snew

time: 79.4 us -> 77.2 us (0.972)
  Pallas kernels: 75.7 us -> 73.5 us
    pallas_call x1, Pallas kernels: 75.7 us -> 73.5 us  [per_device(): pl.pallas_call(kernel, name='coupled_step', out_shape=(jax.ShapeDtypeStru...]
where the time goes in v3:
time: 77.2 us; the launch traced here: 77 us
  Pallas kernels  73.5 us (95%)
  local copies, waits for them, and re-layouts  2.2 us (3%)
  between operations  1.29 us (2%)
    pallas_call x1, Pallas kernels, per_device(): pl.pallas_call(kernel, name='coupled_step', out_shape=(jax.ShapeDtypeStru...  73.5 us
    unnamed x4, local copies, waits for them, and re-layouts  2.2 us

profile of v3, /device:TPU:10, one launch (start us, length us, event | category | flops | bytes accessed | tf_op | source)
XLA Modules:
  0.0 77.0 jit_solution(15325986603871821811)
XLA Ops:
  1.3 73.5 %coupled_step.1 = (f32[6,8,512]{2,1,0:T(8,128)}, f32[8,16,128]{2,1,0:T(8,128)}) custom-call(f32[6,8,512]{2,1,0:T(8,128)} %bitcast.5, f32[8,16,128]{2,1,0:T(8,128)} %sc_far.1, s32[1]{0:T(128)S(6)} %copy.26.off, f32[64,256]{1,0:T(8,128)} %constant.36.clone.rest_0_, f32[64,256]{1,0:T(8,128)} %constant.37.clone.rest_1_, f32[64,128]{1,0:T(8,128)} %constant.38.clone.rest_2_, ...), custom_call_target="tpu_custom_call" | custom-call | tf_op jit(solution)/shard_map/coupled_step/pallas_call | solution.py:542
  74.7 0.0 copy-start
  74.7 1.6 %copy.27 = f32[3,2,1,8,512]{4,3,2,1,0:T(8,128)} copy(f32[3,2,1,8,512]{4,3,2,1,0:T(8,128)} %bitcast.4) | data formatting | bytes 196608
  76.3 0.0 copy-done
  76.3 0.6 copy.28
Async XLA Ops:
  74.7 1.6 %copy-start = (f32[8,16,128]{2,1,0:T(8,128)S(1)}, f32[8,16,128]{2,1,0:T(8,128)}, u32[]{:S(2)}) copy-start(f32[8,16,128]{2,1,0:T(8,128)} %get-tuple-element.11) | copy-start | bytes 196612

commit v4 on v3

--- a/solution.py
+++ b/solution.py
@@ -230,7 +230,7 @@
     n_tables = len(NAMES)
     far_tables, near_tables = rest[:n_tables], rest[-n_tables:]
     rest = rest[:-n_tables]
-    (vnew, snew, send1, recv1, send2, recv2, relay2, send3, recv3, send4, recv4,
+    (push_out, snew, send1, recv1, send2, recv2, relay2, send3, recv3, send4, recv4,
      vsend, vrecv, vlo_s, vhi_s, vlo_r, vhi_r, edge_s, edge_r, rim_s, rim_r, corner_s, corner_r, turned, tile, side, coarse, fine,
      s1, r1, s2, r2, s3, r3, s4, r4, sv, rv, sl, rl, sh, rh, sm, rm, row_sem, vh, sc, load) = rest[n_tables:]
 
@@ -423,7 +423,7 @@
 
         @pl.when(jnp.logical_or(to < 6, to >= 10))
         def _():
-            remote(send4.at[slot], rows(recv4, 16 * w, 16), s4.at[d], r4.at[d], plane_peers[d - 1]).start()
+            remote(send4.at[slot, pl.ds(0, 12)], rows(recv4, 16 * w, 12), s4.at[d], r4.at[d], plane_peers[d - 1]).start()
 
     @pl.when(kept)
     def _():
@@ -464,26 +464,20 @@
 
     row8 = 8 * c + lax.broadcasted_iota(jnp.int32, (8, 128), 0)
     wave_x = jnp.where(row8 < 256, row8, row8 - 512)
-    squared_x = jnp.square(wave_x.astype(jnp.float32) * (1.0 / 256.0))
-    damping, keep = [], []
+    keep = []
     for m in range(4):
         column = 128 * m + lax.broadcasted_iota(jnp.int32, (8, 128), 1)
         wave_y = jnp.where(column < 256, column, column - 512)
-        squared_y = jnp.square(wave_y.astype(jnp.float32) * (1.0 / 256.0))
-        damping.append(jnp.exp(-viscosity * time_step * (squared_x + squared_y)))
         keep.append(jnp.logical_and(3 * jnp.abs(wave_x) < 512, 3 * jnp.abs(wave_y) < 512))
 
     @pl.when(jnp.logical_not(kept))
     def _():
-        for n in range(6):
-            for m in range(4):
-                lanes = slice(128 * m, 128 * m + 128)
-                vnew[n, :, lanes] = damping[m] * vh[n, :, lanes]
+        push_out[...] = jnp.zeros_like(push_out)
 
     @pl.when(kept)
     def _():
         for d in range(1, 16):
-            remote(send4.at[0], rows(recv4, 0, 16), s4.at[d], r4.at[d], plane_peers[d - 1]).wait_recv()
+            remote(send4.at[0, pl.ds(0, 12)], rows(recv4, 0, 12), s4.at[d], r4.at[d], plane_peers[d - 1]).wait_recv()
         gathered = [
             jnp.concatenate([recv4[pl.ds(4 * f + k, 16, stride=16), :] for k in range(4)], axis=0)
             for f in range(3)
@@ -495,9 +489,7 @@
                     lanes = slice(128 * m, 128 * m + 128)
                     push = forcing[f][32 * ri + 8 * m : 32 * ri + 8 * m + 8]
                     n = 2 * f + ri
-                    vnew[n, :, lanes] = damping[m] * (
-                        vh[n, :, lanes] + time_step * jnp.where(keep[m], push, 0.0)
-                    )
+                    push_out[n, :, lanes] = time_step * jnp.where(keep[m], push, 0.0)
 
     for copy in sent1 + sentv + [
         edge_right, edge_left, rim_next, rim_prev, corner_next, corner_prev, far_up, far_down, near_up, near_down,
@@ -509,7 +501,7 @@
 
         @pl.when(jnp.logical_or(to < 6, to >= 10))
         def _():
-            remote(send4.at[0], rows(recv4, 0, 16), s4.at[d], r4.at[d], plane_peers[d - 1]).wait_send()
+            remote(send4.at[0, pl.ds(0, 12)], rows(recv4, 0, 12), s4.at[d], r4.at[d], plane_peers[d - 1]).wait_send()
 
 
 def advance(values, x_speed, y_speed):
@@ -539,7 +531,7 @@
     def buf(*shape):
         return pltpu.VMEM(shape, f32)
 
-    vnew, snew = pl.pallas_call(
+    push, snew = pl.pallas_call(
         kernel,
         name="coupled_step",
         out_shape=(jax.ShapeDtypeStruct((6, 8, 512), f32), jax.ShapeDtypeStruct((8, 16, 128), f32)),
@@ -558,7 +550,14 @@
         ] + [buf(*consts[k].shape) for k in NAMES],
         compiler_params=pltpu.CompilerParams(collective_id=0, has_side_effects=True),
     )(velocity_hat.reshape(6, 8, 512), scalar, tile_offset, *[jnp.asarray(consts[k]) for k in NAMES])
-    return vnew.reshape(3, 2, 1, 8, 512), snew
+    row = 8 * lax.axis_index("col") + jnp.arange(8, dtype=jnp.int32)
+    column = jnp.arange(N, dtype=jnp.int32)
+
+    def squared(index):
+        return jnp.square(jnp.where(index < N // 2, index, index - N).astype(f32) / (N // 2))
+
+    damping = jnp.exp(-viscosity * time_step * (squared(row)[:, None] + squared(column)[None, :]))
+    return damping * (velocity_hat + push.reshape(velocity_hat.shape)), snew
 
 
 def solution(mesh):

time: 77.2 us -> 77.4 us (level)
  other arithmetic: 0 us -> 1.67 us
  local copies, waits for them, and re-layouts: 2.2 us -> 0.64 us
    mul x0 -> x1, other arithmetic: none -> 1.58 us  [per_device(): return (damping * (velocity_hat + push.reshape(velocity_hat.shape)), snew)]
    unnamed x4 -> x5, local copies, waits for them, and re-layouts: 2.2 us -> 0.64 us
where the time goes in v4:
time: 77.4 us; the launch traced here: 77.2 us
  Pallas kernels  73.6 us (95%)
  other arithmetic  1.67 us (2%)
  between operations  1.32 us (2%)
    pallas_call x1, Pallas kernels, per_device(): pl.pallas_call(kernel, name='coupled_step', out_shape=(jax.ShapeDtypeStru...  73.6 us
    mul x1, other arithmetic, per_device(): return (damping * (velocity_hat + push.reshape(velocity_hat.shape)), snew)  1.58 us

profile of v4, /device:TPU:10, one launch (start us, length us, event | category | flops | bytes accessed | tf_op | source)
XLA Modules:
  0.0 77.2 jit_solution(5012104780755915455)
XLA Ops:
  1.3 0.1 multiply_exponential_fusion
  1.4 0.0 copy-start
  1.4 73.6 %coupled_step.1 = (f32[6,8,512]{2,1,0:T(8,128)}, f32[8,16,128]{2,1,0:T(8,128)}) custom-call(f32[6,8,512]{2,1,0:T(8,128)} %bitcast.4, f32[8,16,128]{2,1,0:T(8,128)} %sc_far.1, s32[1]{0:T(128)S(6)} %copy.25.off, f32[64,256]{1,0:T(8,128)} %constant.57.clone.rest_0_, f32[64,256]{1,0:T(8,128)} %constant.58.clone.rest_1_, f32[64,128]{1,0:T(8,128)} %constant.59.clone.rest_2_, ...), custom_call_target="tpu_custom_call" | custom-call | tf_op jit(solution)/shard_map/coupled_step/pallas_call | solution.py:534
  75.0 0.0 copy-done
  75.0 0.0 copy-start.1
  75.0 1.6 %add_multiply_fusion = f32[3,2,1,8,512]{4,3,2,1,0:T(8,128)} fusion(f32[3,2,1,8,512]{4,3,2,1,0:T(8,128)S(1)} %copy-done, f32[3,2,1,8,512]{4,3,2,1,0:T(8,128)} %bitcast.5, f32[8,512]{1,0:T(8,128)S(1)} %multiply_exponential_fusion), kind=kLoop, calls=%fused_computation | loop fusion | flops 49152 | bytes 311296 | tf_op jit(solution)/shard_map/mul | solution.py:560
  76.6 0.0 copy-done.1
  76.6 0.6 copy.26
  (2 shorter events, 0.0 us)
Async XLA Ops:
  1.4 73.6 %copy-start = (f32[3,2,1,8,512]{4,3,2,1,0:T(8,128)S(1)}, f32[3,2,1,8,512]{4,3,2,1,0:T(8,128)}, u32[]{:S(2)}) copy-start(f32[3,2,1,8,512]{4,3,2,1,0:T(8,128)} %param.21) | copy-start | bytes 294916
  75.0 1.6 %copy-start.1 = (f32[8,16,128]{2,1,0:T(8,128)S(1)}, f32[8,16,128]{2,1,0:T(8,128)}, u32[]{:S(2)}) copy-start(f32[8,16,128]{2,1,0:T(8,128)} %get-tuple-element.9) | copy-start | bytes 196612
